TPU v7x, 256 devices: a whole 4x4x8 slice. The times are simulated.
256 devices in a mesh: dp: 128 (over x, z, y_hi, core), outer: 2 (over y_lo).
Axes of the slice: x: 4, y: 4 (y_hi: 2, y_lo: 2; y = y_hi * 2 + y_lo), z: 8, core: 2. Of those that a mesh axis runs over, the one named last changes fastest.
Arguments:
- images: bfloat16 [16384, 1024], P('dp'), may hold values from -8 to 8
- texts: bfloat16 [16384, 1024], P(('dp', 'outer')), may hold values from -8 to 8
- logit_scale: float32 [1], replicated, may hold values from 70 to 100
Outputs:
- image_loss: float32 [16384], P(('dp', 'outer'))
- text_loss: float32 [16384], P(('dp', 'outer'))
All inputs are finite; a program needn't handle non-finite values.
Results may differ from a plain program's by a relative error of at most 0.003.
Values may be sent and summed in bfloat16 or wider, within the bound.
No kernel may reach another device: no remote copies, remote signals or barrier semaphores. Data moves between devices by JAX's collectives and lax.ppermute only.
A program may use at most 64 MiB of HBM per device.

v0:
```python
import jax
import jax.numpy as jnp
from jax import lax
from jax.sharding import PartitionSpec as P


def side_by_side(arrays, axis, split_dim, concat_dim, along):
    ends, at = ([], 0)
    for a in arrays[:-1]:
        at += a.shape[along]
        ends.append(at)
    both = jnp.concatenate(arrays, axis=along)
    return tuple(
        jnp.split(
            lax.all_to_all(both, axis, split_axis=split_dim, concat_axis=concat_dim, tiled=True),
            ends,
            axis=along,
        )
    )


def partner(block, axis, apart):
    count = lax.axis_size(axis)
    route = []
    for low in range(count):
        high = low | 1 << apart
        if high != low and high < count:
            route += [(low, high), (high, low)]
    return lax.ppermute(block, axis, route)


def normalise(features):
    widened = features.astype(jnp.float32)
    return (widened * lax.rsqrt(jnp.sum(widened * widened, axis=1, keepdims=True) + 1.0)).astype(
        jnp.bfloat16
    )


def merge_states(first, second):
    peak = jnp.maximum(first[0], second[0])
    return (peak, first[1] * jnp.exp(first[0] - peak) + second[1] * jnp.exp(second[0] - peak))


def on_device(images, texts, logit_scale):
    image_unit = normalise(images)
    text_unit = normalise(texts)
    factor = logit_scale[0]
    img_rows = image_unit.shape[0]
    txt_rows = text_unit.shape[0]
    cycle_size = lax.axis_size("dp")
    row_peak = jnp.full((img_rows,), -1e30, jnp.float32)
    scores = (
        jnp.einsum(
            "id,jd->ij",
            image_unit,
            lax.all_gather(text_unit, "dp", axis=0, tiled=True),
            preferred_element_type=jnp.float32,
        )
        * factor
    )
    block_peak = jnp.max(scores, axis=0)
    block_total = jnp.sum(jnp.exp(scores - block_peak), axis=0)
    col_peak = block_peak
    col_total = block_total
    new_peak = jnp.maximum(row_peak, jnp.max(scores, axis=1))
    row_total = jnp.sum(jnp.exp(scores - new_peak[:, None]), axis=1)
    row_peak, row_total, col_peak, col_total = (new_peak, row_total, col_peak, col_total)
    peak_table, total_table = side_by_side(
        (col_peak.reshape(cycle_size, txt_rows), col_total.reshape(cycle_size, txt_rows)),
        "dp",
        0,
        0,
        1,
    )
    text_peak = jnp.max(peak_table, axis=0)
    text_total = jnp.sum(total_table * jnp.exp(peak_table - text_peak), axis=0)
    text_lse = text_peak + jnp.log(text_total)
    outer_index = lax.axis_index("outer")
    group_count = img_rows // txt_rows
    peak_halves = row_peak.reshape(group_count, txt_rows)
    total_halves = row_total.reshape(group_count, txt_rows)
    own_half = (
        lax.dynamic_index_in_dim(peak_halves, outer_index, 0, keepdims=False),
        lax.dynamic_index_in_dim(total_halves, outer_index, 0, keepdims=False),
    )
    partner_half = (
        lax.dynamic_index_in_dim(peak_halves, 1 - outer_index, 0, keepdims=False),
        lax.dynamic_index_in_dim(total_halves, 1 - outer_index, 0, keepdims=False),
    )
    received = partner((partner_half[0], partner_half[1]), "outer", 0)
    image_peak, image_total = merge_states(own_half, received)
    image_own = lax.dynamic_slice_in_dim(image_unit, outer_index * txt_rows, txt_rows, 0)
    diagonal = (
        jnp.sum(image_own.astype(jnp.float32) * text_unit.astype(jnp.float32), axis=1) * factor
    )
    return (image_peak + jnp.log(image_total) - diagonal, text_lse - diagonal)


def solution(mesh):
    in_specs = (P("dp", None), P(("dp", "outer"), None), P())
    out_specs = (P(("dp", "outer")), P(("dp", "outer")))
    return jax.shard_map(
        on_device, mesh=mesh, in_specs=in_specs, out_specs=out_specs, check_vma=False
    )
```

profile of v0, /device:TPU:1, one launch (start us, length us, event | category | flops | bytes accessed | tf_op | source)
XLA Modules:
  0.0 210.6 jit_solution(15811068224282388094)
XLA Ops:
  7.2 0.0 all-gather.2.cloned.1.call-start
  7.2 1.1 fusion
  8.3 1.1 fusion.1
  9.4 1.0 fusion.2
  10.4 1.8 multiply_reduce_fusion
  12.2 0.0 all-gather.2.cloned.1.call-update
  12.9 151.6 %all-gather.2.cloned.1.call-done = bf16[8192,1024]{1,0:T(8,128)(2,1)} async-done(((bf16[64,1024]{1,0:T(8,128)(2,1)}), bf16[8192,1024]{1,0:T(8,128)(2,1)}) %all-gather.2.cloned.1.call-update) | async-done | bytes 16777232 | tf_op jit(solution)/shard_map/all_gather | solution.py:56
  164.5 13.3 %fusion.12 = (f32[8192]{0:T(1024)S(1)}, f32[128]{0:T(128)S(1)}, f32[128,8192]{1,0:T(8,128)}) fusion(f32[]{:T(128)} %bitcast.23, bf16[128,1024]{1,0:T(8,128)(2,1)S(1)} %fusion.1, bf16[8192,1024]{1,0:T(8,128)(2,1)} %all-gather.2.cloned.1.call-done), kind=kOutput, calls=%fused_computation.33 | convolution fusion | flops 2150621184 | bytes 21266948 | tf_op jit(solution)/shard_map/id,jd->ij/dot_general | solution.py:53
  177.8 0.1 reshape.37
  177.9 3.5 %exponential_reduce_fusion = (f32[8192]{0:T(1024)S(1)}, f32[128]{0:T(128)S(1)}) fusion(f32[128,8192]{1,0:T(8,128)} %get-tuple-element.10, f32[8192]{0:T(1024)S(1)} %get-tuple-element.4, f32[128]{0:T(128)S(1)} %broadcast_maximum_fusion), kind=kLoop, calls=%fused_computation.1 | loop fusion | flops 4185984 | bytes 4260864 | tf_op jit(solution)/shard_map/reduce_sum | solution.py:62
  181.4 0.1 reshape.38
  181.5 0.7 pad_maximum_fusion
  182.2 8.8 %all-to-all-start = ((f32[128,1,128]{2,1,0:T(1,128)}), f32[128,1,128]{2,1,0:T(1,128)S(1)}, u32[]{:S(2)}, u32[]{:S(2)}) async-start(f32[128,1,128]{2,1,0:T(1,128)} %bitcast.6), calls=%async_computation | async-start | bytes 131072 | tf_op jit(solution)/shard_map/all_to_all | solution.py:15
  191.0 0.1 reshape.36
  191.1 0.1 max_broadcast_in_dim.12
  191.1 1.2 collective-permute-start.1
  192.3 0.3 collective-permute-start
  192.6 10.4 %all-to-all-done = f32[128,1,128]{2,1,0:T(1,128)S(1)} async-done(((f32[128,1,128]{2,1,0:T(1,128)}), f32[128,1,128]{2,1,0:T(1,128)S(1)}, u32[]{:S(2)}, u32[]{:S(2)}) %all-to-all-start) | async-done | bytes 65568 | tf_op jit(solution)/shard_map/all_to_all | solution.py:15
  203.1 0.1 fusion.4
  203.2 0.0 collective-permute-done.1
  203.2 0.0 collective-permute-done
  203.2 0.5 add_subtract_fusion
  (6 shorter events, 0.1 us)
Async XLA Ops:
  7.2 157.3 %all-gather.2.cloned.1.call-start = ((), (), s32[]{:S(2)}) async-start(), calls=%async_computation.1 | async-start | bytes 16908288 | tf_op jit(solution)/shard_map/all_gather | solution.py:56
  182.2 20.9 %all-to-all-start = ((f32[128,1,128]{2,1,0:T(1,128)}), f32[128,1,128]{2,1,0:T(1,128)S(1)}, u32[]{:S(2)}, u32[]{:S(2)}) async-start(f32[128,1,128]{2,1,0:T(1,128)} %bitcast.6), calls=%async_computation | async-start | bytes 131072 | tf_op jit(solution)/shard_map/all_to_all | solution.py:15
  191.1 12.1 %collective-permute-start.1 = (f32[64]{0:T(128)S(1)}, f32[64]{0:T(128)S(1)}, u32[]{:S(2)}, u32[]{:S(2)}) collective-permute-start(f32[64]{0:T(128)S(1)} %fusion.10), channel_id=1, source_target_pairs={{0,1},{1,0},{2,3},{3,2},{4,5},{5,4},{6,7},{7,6},{8,9},{9,8},{10,11... | collective-permute-start | bytes 776 | tf_op jit(solution)/shard_map/ppermute | solution.py:29
  192.3 10.9 %collective-permute-start = (f32[64]{0:T(128)S(1)}, f32[64]{0:T(128)S(1)}, u32[]{:S(2)}, u32[]{:S(2)}) collective-permute-start(f32[64]{0:T(128)S(1)} %fusion.6), channel_id=1, source_target_pairs={{0,1},{1,0},{2,3},{3,2},{4,5},{5,4},{6,7},{7,6},{8,9},{9,8},{10,11... | collective-permute-start | bytes 776 | tf_op jit(solution)/shard_map/ppermute | solution.py:29
Sparse Core Ops, SparseCore 0:
  12.3 152.1 all-gather.1
where the time goes:
time: 211 us
  waiting for transfers between devices  162 us (77%)
  between operations  14.7 us (7%)
  matrix products  13.3 us (6%)
  starting transfers between devices  10.3 us (5%)
  other arithmetic  9.85 us (5%)
    all_gather x1, waiting for transfers between devices, on_device(): lax.all_gather(text_unit, 'dp', axis=0, tiled=True)  152 us
    dot_general x1, matrix products, on_device(): jnp.einsum('id,jd->ij', image_unit, lax.all_gather(text_unit, 'dp', axis=...  13.3 us
    all_to_all x1, waiting for transfers between devices, side_by_side(): lax.all_to_all(both, axis, split_axis=split_dim, concat_axis=concat_dim,...  10.4 us
    all_to_all x1, starting transfers between devices, side_by_side(): lax.all_to_all(both, axis, split_axis=split_dim, concat_axis=concat_dim,...  8.76 us
  transfers between devices with their start and end apart: 4, of which 2 were waited for; matrix products, arithmetic and copies ran while one was open for 0% of the time, Pallas kernels for 0%

commit v1 on v0

--- a/solution.py
+++ b/solution.py
@@ -53,7 +53,9 @@
         jnp.einsum(
             "id,jd->ij",
             image_unit,
-            lax.all_gather(text_unit, "dp", axis=0, tiled=True),
+            jnp.concatenate(
+                lax.all_to_all(jnp.stack([text_unit] * lax.axis_size("dp")), "dp", 0, 0), axis=0
+            ),
             preferred_element_type=jnp.float32,
         )
         * factor

time: 211 us -> 434 us (2.06)
  waiting for transfers between devices: 162 us -> 375 us
  starting transfers between devices: 10.3 us -> 29.2 us
  between operations: 14.7 us -> 1.34 us
  local copies, waits for them, and re-layouts: 0.32 us -> 6.36 us
    all_to_all x0 -> x1, waiting for transfers between devices: none -> 364 us  [on_device(): lax.all_to_all(jnp.stack([text_unit] * lax.axis_size('dp')), 'dp', 0, 0)]
    all_gather x1 -> x0, waiting for transfers between devices: 152 us -> none  [on_device(): lax.all_gather(text_unit, 'dp', axis=0, tiled=True)]
    all_to_all x0 -> x1, starting transfers between devices: none -> 16.8 us  [on_device(): lax.all_to_all(jnp.stack([text_unit] * lax.axis_size('dp')), 'dp', 0, 0)]
    another operation x0 -> x1, local copies, waits for them, and re-layouts: none -> 6.04 us  [on_device(): jnp.stack([text_unit] * lax.axis_size('dp'))]
where the time goes in v1:
time: 434 us
  waiting for transfers between devices  375 us (86%)
  starting transfers between devices  29.2 us (7%)
  matrix products  13.3 us (3%)
  other arithmetic  9.21 us (2%)
  local copies, waits for them, and re-layouts  6.36 us (1%)
    all_to_all x1, waiting for transfers between devices, on_device(): lax.all_to_all(jnp.stack([text_unit] * lax.axis_size('dp')), 'dp', 0, 0)  364 us
    all_to_all x1, starting transfers between devices, on_device(): lax.all_to_all(jnp.stack([text_unit] * lax.axis_size('dp')), 'dp', 0, 0)  16.8 us
    dot_general x1, matrix products, on_device(): jnp.einsum('id,jd->ij', image_unit, jnp.concatenate(lax.all_to_all(jnp.st...  13.3 us
    all_to_all x1, starting transfers between devices, side_by_side(): lax.all_to_all(both, axis, split_axis=split_dim, concat_axis=concat_dim,...  10.9 us
    all_to_all x1, waiting for transfers between devices, side_by_side(): lax.all_to_all(both, axis, split_axis=split_dim, concat_axis=concat_dim,...  10.4 us
  transfers between devices with their start and end apart: 4, of which 2 were waited for; matrix products, arithmetic and copies ran while one was open for 0% of the time, Pallas kernels for 0%

profile of v1, /device:TPU:1, one launch (start us, length us, event | category | flops | bytes accessed | tf_op | source)
XLA Modules:
  0.0 434.1 jit_solution(14180775593307750168)
XLA Ops:
  0.6 1.1 fusion
  1.7 1.1 fusion.1
  2.8 1.0 fusion.2
  3.8 1.1 multiply_reduce_fusion
  5.0 6.0 %stack.2 = bf16[128,64,1024]{2,1,0:T(8,128)(2,1)} broadcast(bf16[64,1024]{1,0:T(8,128)(2,1)S(1)} %get-tuple-element.7), dimensions={1,2} | broadcast | bytes 16908288 | tf_op jit(solution)/shard_map/stack | solution.py:57
  11.0 16.8 %all-to-all-start = ((bf16[128,64,1024]{2,1,0:T(8,128)(2,1)}), bf16[128,64,1024]{2,1,0:T(8,128)(2,1)}, u32[]{:S(2)}, u32[]{:S(2)}) async-start(bf16[128,64,1024]{2,1,0:T(8,128)(2,1)} %stack.2), calls=%async_computation | async-start | bytes 33554432 | tf_op jit(solution)/shard_map/all_to_all | solution.py:57
  28.5 364.2 %all-to-all-done = bf16[128,64,1024]{2,1,0:T(8,128)(2,1)} async-done(((bf16[128,64,1024]{2,1,0:T(8,128)(2,1)}), bf16[128,64,1024]{2,1,0:T(8,128)(2,1)}, u32[]{:S(2)}, u32[]{:S(2)}) %all-to-all-start) | async-done | bytes 16777248 | tf_op jit(solution)/shard_map/all_to_all | solution.py:57
  392.8 13.3 %fusion.12 = (f32[8192]{0:T(1024)S(1)}, f32[128]{0:T(128)S(1)}, f32[128,8192]{1,0:T(8,128)}) fusion(f32[]{:T(128)} %bitcast.24, bf16[128,1024]{1,0:T(8,128)(2,1)S(1)} %fusion.1, bf16[8192,1024]{1,0:T(8,128)(2,1)} %bitcast), kind=kOutput, calls=%fused_computation.33 | convolution fusion | flops 2150621184 | bytes 21266948 | tf_op jit(solution)/shard_map/id,jd->ij/dot_general | solution.py:53
  406.1 0.1 reshape.43
  406.2 3.5 exponential_reduce_fusion
  409.7 0.1 reshape.44
  409.7 0.7 pad_maximum_fusion
  410.4 10.9 %all-to-all-start.1 = ((f32[128,1,128]{2,1,0:T(1,128)}), f32[128,1,128]{2,1,0:T(1,128)S(1)}, u32[]{:S(2)}, u32[]{:S(2)}) async-start(f32[128,1,128]{2,1,0:T(1,128)} %bitcast.7), calls=%async_computation.1 | async-start | bytes 131072 | tf_op jit(solution)/shard_map/all_to_all | solution.py:15
  421.3 0.1 reshape.42
  421.4 0.1 max_broadcast_in_dim.12
  421.5 0.4 collective-permute-start.1
  421.9 1.1 collective-permute-start
  423.0 10.4 %all-to-all-done.1 = f32[128,1,128]{2,1,0:T(1,128)S(1)} async-done(((f32[128,1,128]{2,1,0:T(1,128)}), f32[128,1,128]{2,1,0:T(1,128)S(1)}, u32[]{:S(2)}, u32[]{:S(2)}) %all-to-all-start.1) | async-done | bytes 65568 | tf_op jit(solution)/shard_map/all_to_all | solution.py:15
  433.5 0.1 fusion.4
  433.6 0.0 collective-permute-done.1
  433.6 0.0 collective-permute-done
  433.6 0.5 add_subtract_fusion
  (6 shorter events, 0.1 us)
Async XLA Ops:
  11.0 381.7 %all-to-all-start = ((bf16[128,64,1024]{2,1,0:T(8,128)(2,1)}), bf16[128,64,1024]{2,1,0:T(8,128)(2,1)}, u32[]{:S(2)}, u32[]{:S(2)}) async-start(bf16[128,64,1024]{2,1,0:T(8,128)(2,1)} %stack.2), calls=%async_computation | async-start | bytes 33554432 | tf_op jit(solution)/shard_map/all_to_all | solution.py:57
  410.4 23.0 %all-to-all-start.1 = ((f32[128,1,128]{2,1,0:T(1,128)}), f32[128,1,128]{2,1,0:T(1,128)S(1)}, u32[]{:S(2)}, u32[]{:S(2)}) async-start(f32[128,1,128]{2,1,0:T(1,128)} %bitcast.7), calls=%async_computation.1 | async-start | bytes 131072 | tf_op jit(solution)/shard_map/all_to_all | solution.py:15
  421.5 12.1 %collective-permute-start.1 = (f32[64]{0:T(128)S(1)}, f32[64]{0:T(128)S(1)}, u32[]{:S(2)}, u32[]{:S(2)}) collective-permute-start(f32[64]{0:T(128)S(1)} %fusion.10), channel_id=1, source_target_pairs={{0,1},{1,0},{2,3},{3,2},{4,5},{5,4},{6,7},{7,6},{8,9},{9,8},{10,11... | collective-permute-start | bytes 776 | tf_op jit(solution)/shard_map/ppermute | solution.py:29
  421.9 11.6 %collective-permute-start = (f32[64]{0:T(128)S(1)}, f32[64]{0:T(128)S(1)}, u32[]{:S(2)}, u32[]{:S(2)}) collective-permute-start(f32[64]{0:T(128)S(1)} %fusion.6), channel_id=1, source_target_pairs={{0,1},{1,0},{2,3},{3,2},{4,5},{5,4},{6,7},{7,6},{8,9},{9,8},{10,11... | collective-permute-start | bytes 776 | tf_op jit(solution)/shard_map/ppermute | solution.py:29
